TPU v7x, 256 devices: a whole 4x4x8 slice. The times are simulated.
256 devices in a mesh: dp: 32 (over y, z_lo, x), tensor: 8 (over z_hi, core).
Axes of the slice: x: 4, y: 4, z: 8 (z_hi: 4, z_lo: 2; z = z_hi * 2 + z_lo), core: 2. Of those that a mesh axis runs over, the one named last changes fastest.
Arguments:
- hidden: bfloat16 [32768, 7168], P('dp', 'tensor'), parts along dimension 0, may hold values from -6 to 6
- w_dq: bfloat16 [7168, 1536], P('tensor'), may hold values from -0.0625 to 0.0625
- w_dkv: bfloat16 [7168, 576], P('tensor'), may hold values from -0.0625 to 0.0625
- q_gain: float32 [1536], replicated, may hold values from 0.1 to 1.9
- kv_gain: float32 [512], replicated, may hold values from 0.1 to 1.9
- w_uq: bfloat16 [1536, 12288], P(None, 'tensor'), may hold values from -0.15625 to 0.15625
- w_ukv: bfloat16 [512, 16384], P(None, 'tensor'), may hold values from -0.25 to 0.25
Outputs:
- queries: bfloat16 [32768, 12288], P('dp', 'tensor'), parts along dimension 0
- keys_values: bfloat16 [32768, 16384], P('dp', 'tensor'), parts along dimension 0
- rotary_key: bfloat16 [32768, 64], P(('dp', 'tensor')), parts along dimension 0
There are 32 independent parts, one for each index of `dp`. A program takes and returns all parts, laid end to end along the dimension named above; an argument that names none is the same for every part. Nothing has to cross between parts.
All inputs are finite; a program needn't handle non-finite values.
Results may differ from a plain program's by a relative error of at most 0.0049.
Values may be sent and summed in bfloat16 or wider, within the bound.
A program may use at most 128 MiB of HBM per device.

v0:
```python
import jax
import jax.numpy as jnp
from jax import lax
from jax.sharding import PartitionSpec as P

NOPE = 128
ROPE = 64


def rotate(values, angle):
    half = values.shape[-1] // 2
    first = values[..., :half]
    second = values[..., half:]
    cosine = jnp.cos(angle)
    sine = jnp.sin(angle)
    return jnp.concatenate(
        [first * cosine - second * sine, second * cosine + first * sine], axis=-1
    )


def angles(first_row, count, half):
    positions = (first_row + lax.iota(jnp.int32, count)).astype(jnp.float32)
    freqs = 50000.0 ** (-jnp.arange(half, dtype=jnp.float32) / half)
    return positions[:, None] * freqs[None, :]


def normalize(block, gain):
    scale = lax.rsqrt(jnp.mean(block * block, axis=1, keepdims=True) + 1e-06)
    return (block * scale * gain[None, :]).astype(jnp.bfloat16)


def shards(hidden, w_dq, w_dkv, q_gain, kv_gain, w_uq, w_ukv):
    q_width = w_dq.shape[1]
    kv_width = kv_gain.shape[0]
    rope_width = w_dkv.shape[1] - kv_width
    head_width = NOPE + ROPE
    local_heads = w_uq.shape[1] // head_width
    total_rows = hidden.shape[0]
    share = total_rows // lax.axis_size("tensor")
    own_start = lax.axis_index("tensor") * share
    down = lax.psum_scatter(
        jnp.concatenate(
            [
                jnp.dot(hidden, w_dq, preferred_element_type=jnp.float32),
                jnp.dot(hidden, w_dkv, preferred_element_type=jnp.float32),
            ],
            axis=1,
        ),
        "tensor",
        scatter_dimension=0,
        tiled=True,
    )
    latent = jnp.concatenate(
        [
            normalize(down[:, :q_width], q_gain),
            normalize(down[:, q_width : q_width + kv_width], kv_gain),
        ],
        axis=1,
    )
    piece = lax.all_gather(latent, "tensor", axis=0, tiled=True)
    count = piece.shape[0]
    query_full = jnp.dot(piece[:, :q_width], w_uq, preferred_element_type=jnp.float32)
    query_full = query_full.reshape(count, local_heads, head_width)
    angle = angles(jnp.int32(0), count, ROPE // 2)
    turned = rotate(query_full[:, :, NOPE:], angle[:, None, :])
    query_out = jnp.concatenate([query_full[:, :, :NOPE], turned], axis=2)
    query_out = query_out.reshape(count, local_heads * head_width).astype(jnp.bfloat16)
    kv_out = jnp.dot(piece[:, q_width:], w_ukv, preferred_element_type=jnp.float32).astype(
        jnp.bfloat16
    )
    both = jnp.concatenate([query_out, kv_out], axis=1)
    mine = down[:, q_width + kv_width :]
    rotary_key = rotate(mine, angles(own_start, share, rope_width // 2)).astype(jnp.bfloat16)
    query_cols = local_heads * head_width
    return (both[:, :query_cols], both[:, query_cols:], rotary_key)


def solution(mesh):
    in_specs = (
        P("dp", "tensor"),
        P("tensor", None),
        P("tensor", None),
        P(),
        P(),
        P(None, "tensor"),
        P(None, "tensor"),
    )
    out_specs = (P("dp", "tensor"), P("dp", "tensor"), P(("dp", "tensor"), None))
    return jax.shard_map(shards, mesh=mesh, in_specs=in_specs, out_specs=out_specs, check_vma=False)
```

profile of v0, /device:TPU:43, one launch (start us, length us, event | category | flops | bytes accessed | tf_op | source)
XLA Modules:
  0.0 216.0 jit_solution(12857306435849263300)
XLA Ops:
  7.2 0.0 copy-start
  7.2 0.0 reduce-scatter.2.cloned.1.call-start
  7.2 1.7 copy-done
  8.9 0.0 copy-start.3
  9.0 0.0 copy-start.4
  9.0 5.2 %fusion.11 = f32[1024,1536]{0,1:T(8,128)S(1)} fusion(bf16[1024,896]{1,0:T(8,128)(2,1)} %param.7, bf16[896,1536]{1,0:T(8,128)(2,1)S(1)} %copy-done), kind=kOutput, calls=%fused_computation.32 | convolution fusion | flops 2818572288 | bytes 10878976 | tf_op jit(solution)/shard_map/dot_general | solution.py:44
  14.2 0.0 copy-done.3
  14.2 0.0 copy-done.4
  14.2 2.8 %fusion.12 = f32[1024,576]{0,1:T(8,128)} fusion(bf16[1024,896]{1,0:T(8,128)(2,1)S(1)} %copy-done.3, bf16[896,576]{0,1:T(8,128)(2,1)S(1)} %copy-done.4), kind=kOutput, calls=%fused_computation.33 | convolution fusion | flops 1056964608 | bytes 5226496 | tf_op jit(solution)/shard_map/dot_general | solution.py:45
  17.0 6.4 %pad_maximum_fusion = f32[1024,2112]{0,1:T(8,128)} fusion(f32[1024,576]{0,1:T(8,128)} %fusion.12, f32[1024,1536]{0,1:T(8,128)S(1)} %fusion.11), kind=kLoop, calls=%fused_computation | loop fusion | flops 2162688 | bytes 17301504 | tf_op jit(solution)/shard_map/concatenate | solution.py:42
  23.4 0.0 copy-start.1
  23.4 0.0 copy-start.2
  23.4 0.0 reduce-scatter.2.cloned.1.call-update
  23.4 0.2 all-gather.2.cloned.1.call-start
  23.7 98.7 %reduce-scatter.2.cloned.1.call-done = f32[128,2112]{0,1:T(8,128)} async-done(((f32[1024,2112]{0,1:T(8,128)}), f32[128,2112]{0,1:T(8,128)}) %reduce-scatter.2.cloned.1.call-update) | async-done | bytes 1081360 | tf_op jit(solution)/shard_map/reduce_scatter | solution.py:41
  122.3 1.3 multiply_reduce_fusion
  123.7 1.0 multiply_reduce_fusion.1
  124.7 0.0 copy-done.1
  124.7 1.4 multiply_convert_fusion
  126.1 0.0 copy-done.2
  126.2 1.1 multiply_convert_fusion.1
  127.2 0.8 pad_maximum_fusion.2
  128.1 0.0 all-gather.2.cloned.1.call-update
  128.1 0.5 multiply_cosine_fusion
  128.7 0.9 fusion.8
  129.6 0.6 pad_maximum_fusion.3
  130.2 57.4 %all-gather.2.cloned.1.call-done = bf16[1024,2048]{0,1:T(8,128)(2,1)} async-done(((bf16[128,2048]{0,1:T(8,128)(2,1)}), bf16[1024,2048]{0,1:T(8,128)(2,1)}) %all-gather.2.cloned.1.call-update) | async-done | bytes 4194320 | tf_op jit(solution)/shard_map/all_gather | solution.py:60
  187.5 8.1 %fusion = f32[1024,1536]{0,1:T(8,128)S(1)} fusion(bf16[1536,1536]{1,0:T(8,128)(2,1)} %param.12, bf16[1024,2048]{0,1:T(8,128)(2,1)} %all-gather.2.cloned.1.call-done), kind=kOutput, calls=%fused_computation.3 | convolution fusion | flops 4831838208 | bytes 14155776 | tf_op jit(solution)/shard_map/dot_general | solution.py:62
  195.7 0.3 slice.69
  196.0 0.3 subtract_convert_fusion
  196.4 1.9 pad_maximum_fusion.1
  198.2 4.6 %copy.18 = bf16[1024,1536]{1,0:T(8,128)(2,1)} copy(bf16[1024,1536]{0,1:T(8,128)(2,1)} %bitcast.8) | data formatting | bytes 6291456
  202.9 6.3 %convolution_convert_fusion = bf16[1024,2048]{1,0:T(8,128)(2,1)} fusion(bf16[512,2048]{1,0:T(8,128)(2,1)} %param.13, bf16[1024,2048]{0,1:T(8,128)(2,1)} %all-gather.2.cloned.1.call-done), kind=kOutput, calls=%fused_computation.2 | convolution fusion | flops 2149580800 | bytes 7340032 | tf_op jit(solution)/shard_map/dot_general | solution.py:68
  (5 shorter events, 0.0 us)
Async XLA Ops:
  7.2 1.8 copy-start
  7.2 115.2 %reduce-scatter.2.cloned.1.call-start = ((), (), s32[]{:S(2)}) async-start(), calls=%async_computation.1 | async-start | bytes 9732096 | tf_op jit(solution)/shard_map/reduce_scatter | solution.py:41
  8.9 5.2 %copy-start.3 = (bf16[1024,896]{1,0:T(8,128)(2,1)S(1)}, bf16[1024,896]{1,0:T(8,128)(2,1)}, u32[]{:S(2)}) copy-start(bf16[1024,896]{1,0:T(8,128)(2,1)} %param.7) | copy-start | bytes 5505028
  9.0 5.2 %copy-start.4 = (bf16[896,576]{0,1:T(8,128)(2,1)S(1)}, bf16[896,576]{0,1:T(8,128)(2,1)}, u32[]{:S(2)}) copy-start(bf16[896,576]{0,1:T(8,128)(2,1)} %param.9) | copy-start | bytes 3096580
  23.4 101.3 %copy-start.1 = (f32[1536]{0:T(1024)S(1)}, f32[1536]{0:T(1024)}, u32[]{:S(2)}) copy-start(f32[1536]{0:T(1024)} %param.10) | copy-start | bytes 18436
  23.4 102.7 %copy-start.2 = (f32[512]{0:T(512)S(1)}, f32[512]{0:T(512)}, u32[]{:S(2)}) copy-start(f32[512]{0:T(512)} %param.11) | copy-start | bytes 6148
  23.4 164.1 %all-gather.2.cloned.1.call-start = ((), (), s32[]{:S(2)}) async-start(), calls=%async_computation.2 | async-start | bytes 4718592 | tf_op jit(solution)/shard_map/all_gather | solution.py:60
Sparse Core Ops, SparseCore 0:
  23.6 98.7 reduce-scatter.1
  128.2 59.2 all-gather.1
where the time goes:
time: 219 us; the launch traced here: 216 us
  waiting for transfers between devices  156 us (71%)
  matrix products  22.5 us (10%)
  other arithmetic  16.4 us (7%)
  between operations  14.1 us (6%)
  local copies, waits for them, and re-layouts  6.69 us (3%)
    reduce_scatter x1, waiting for transfers between devices, shards(): lax.psum_scatter(jnp.concatenate([jnp.dot(hidden, w_dq, preferred_element...  98.7 us
    all_gather x1, waiting for transfers between devices, shards(): piece = lax.all_gather(latent, 'tensor', axis=0, tiled=True)  57.4 us
    dot_general x1, matrix products, shards(): jnp.dot(piece[:, :q_width], w_uq, preferred_element_type=jnp.float32)  8.14 us
    concatenate x1, other arithmetic, shards(): jnp.concatenate([jnp.dot(hidden, w_dq, preferred_element_type=jnp.float32...  6.4 us
    unnamed x11, local copies, waits for them, and re-layouts  6.37 us
    dot_general x1, matrix products, shards(): jnp.dot(piece[:, q_width:], w_ukv, preferred_element_type=jnp.float32)  6.32 us
    dot_general x1, matrix products, shards(): jnp.dot(hidden, w_dq, preferred_element_type=jnp.float32)  5.2 us
  transfers between devices with their start and end apart: 2, of which 2 were waited for; matrix products, arithmetic and copies ran while one was open for 1% of the time, Pallas kernels for 0%

commit v1 on v0

v1 whole, which is shorter than its diff:
```python
import functools

import jax
import jax.numpy as jnp
import numpy as np
from jax import lax
from jax.experimental import pallas as pl
from jax.experimental.pallas import tpu as pltpu
from jax.sharding import PartitionSpec as P

NOPE = 128
ROPE = 64
CHIPS = 4
PIECES = 4
MESH = pl.DeviceIdType.MESH
F32 = jnp.float32
BF16 = jnp.bfloat16


def rotary_tables(count):
    half = ROPE // 2
    freqs = (50000.0 ** (-np.arange(half, dtype=np.float32) / half)).astype(np.float32)
    angle = np.arange(count, dtype=np.float32)[:, None] * freqs[None, :]
    cosine = np.cos(angle.astype(np.float64)).astype(np.float32)
    sine = np.sin(angle.astype(np.float64)).astype(np.float32)
    cosine = np.tile(cosine, (1, 4))
    sine = np.concatenate([-sine, sine, -sine, sine], axis=1)
    return np.stack([cosine, sine])


def kernel(
    hidden, w_dq, w_dkv, q_gain, kv_gain, w_uq, w_ukv, table,
    q_out, kv_out, key_out,
    hid, wdq, wdkv, qg, kvg, wuq, wukv, tab,
    acc, pair_out, pair_in, ring_out, ring_in, lat, qbuf, kvbuf, keybuf,
    load_sem, pair_s, pair_r, rs_s, rs_r, ag_s, ag_r, fw_s, fw_r, out_sem,
):
    rows = hid.shape[0]
    q_width = wdq.shape[1]
    kv_width = kvg.shape[1]
    down_width = q_width + wdkv.shape[1]
    latent_width = q_width + kv_width
    block = rows // (2 * CHIPS)
    half = block // 2
    piece = half // PIECES
    me = lax.axis_index("tensor")
    chip = me // 2
    core = me - 2 * chip
    partner = me + 1 - 2 * core

    def chip_at(j):
        return lax.rem(chip + j, CHIPS)

    neighbour = (chip_at(1) * 2 + core, chip_at(CHIPS - 1) * 2 + core)
    toward = (1, CHIPS - 1)
    behind = (CHIPS - 1, 1)
    opposite = 2

    def load(i, src, dst):
        return pltpu.make_async_copy(src, dst, load_sem.at[i])

    def chip_rows(j):
        return pl.ds(pl.multiple_of(chip_at(j) * 2 * block, 2 * block), 2 * block)

    hid_loads = [load(j, hidden.at[chip_rows(j)], hid.at[chip_rows(j)]) for j in range(CHIPS)]
    first_loads = [load(4, w_dq, wdq), load(5, w_dkv, wdkv)]
    late_loads = [
        load(6, q_gain, qg), load(7, kv_gain, kvg), load(8, table, tab),
        load(9, w_uq, wuq), load(10, w_ukv, wukv),
    ]
    hid_loads[opposite].start()
    for copy in first_loads:
        copy.start()
    for j in (1, 3, 0):
        hid_loads[j].start()

    barrier = pltpu.get_barrier_semaphore()
    for device in (*neighbour, partner):
        pl.semaphore_signal(barrier, inc=1, device_id={"tensor": device}, device_id_type=MESH)

    def remote(src, dst, send, recv, device):
        return pltpu.make_async_remote_copy(
            src_ref=src, dst_ref=dst, send_sem=send, recv_sem=recv,
            device_id={"tensor": device}, device_id_type=MESH,
        )

    def down(j):
        base = chip_at(j) * 2 * block
        other = pl.ds(pl.multiple_of(base + (1 - core) * block, block), block)
        own = pl.ds(pl.multiple_of(base + core * block, block), block)

        def emit(start, width, weights):
            x = jnp.concatenate([hid[other, :], hid[own, :]], axis=0)
            r = jnp.dot(x, weights, preferred_element_type=F32)
            pair_out[j, :, pl.ds(start, width)] = r[:block].astype(BF16)
            acc[j, :, pl.ds(start, width)] = r[block:]

        @pl.loop(0, 3)
        def _(i):
            start = pl.multiple_of(i * (q_width // 3), 128)
            emit(start, q_width // 3, wdq[:, pl.ds(start, q_width // 3)])

        emit(q_width, kv_width, wdkv[:, :kv_width])
        emit(latent_width, ROPE, wdkv[:, kv_width:])

    pair_copies = [
        remote(pair_out.at[j], pair_in.at[j], pair_s.at[j], pair_r.at[j], partner)
        for j in range(CHIPS)
    ]

    def piece_rows(h, p):
        return pl.ds(h * half + p * piece, piece)

    def chip_sum(j, h, p):
        return acc[j, piece_rows(h, p), :] + pair_in[j, piece_rows(h, p), :].astype(F32)

    def ring_copy(d, stage, p):
        at = pl.ds(p * piece, piece)
        return remote(
            ring_out.at[d, stage, at], ring_in.at[d, stage, at],
            rs_s.at[d, stage, p], rs_r.at[d, stage, p], neighbour[d],
        )

    def ring_got(d, stage, p):
        return ring_in[d, stage, pl.ds(p * piece, piece), :].astype(F32)

    def ring_put(d, stage, p, value):
        ring_out[d, stage, pl.ds(p * piece, piece), :] = value.astype(BF16)

    def lat_rows(j, c, h, p):
        start = (chip_at(j) * 2 + c) * block + h * half + p * piece
        return pl.ds(pl.multiple_of(start, piece), piece)

    def gather_copy(d, stage, p):
        j = (0, 0, behind[d])[stage]
        h = (d, 1 - d, d)[stage]
        at = lat.at[lat_rows(j, core, h, p)]
        return remote(at, at, ag_s.at[d, stage, p], ag_r.at[d, stage, p], neighbour[d])

    def gather_wait(d, stage, p):
        j = (behind[d], behind[d], opposite)[stage]
        h = (d, 1 - d, d)[stage]
        at = lat.at[lat_rows(j, core, h, p)]
        remote(at, at, ag_s.at[d, stage, p], ag_r.at[d, stage, p], neighbour[d]).wait_recv()

    def forward(j, h, p):
        at = lat.at[lat_rows(j, core, h, p)]
        return remote(at, at, fw_s.at[j, h, p], fw_r.at[j, h, p], partner)

    def forward_wait(j):
        for h in range(2):
            for p in range(PIECES):
                at = lat.at[lat_rows(j, 1 - core, h, p)]
                remote(at, at, fw_s.at[j, h, p], fw_r.at[j, h, p], partner).wait_recv()

    lane = lax.broadcasted_iota(jnp.int32, (1, 128), 1)
    low = lax.rem(lane, ROPE) < ROPE // 2

    def turn(x, cosine, sine):
        swapped = jnp.where(low, pltpu.roll(x, 128 - ROPE // 2, 1), pltpu.roll(x, ROPE // 2, 1))
        return x * cosine + swapped * sine

    def up(j):
        at = chip_rows(j)
        cosine = tab[0, at, :]
        sine = tab[1, at, :]
        pair = 2 * (NOPE + ROPE)

        @pl.loop(0, 2)
        def _(i):
            start = pl.multiple_of(i * 2 * pair, 128)
            r = jnp.dot(lat[at, :q_width], wuq[:, pl.ds(start, 2 * pair)], preferred_element_type=F32)
            for k in range(2):
                x0 = r[:, k * pair : k * pair + 128]
                x1 = r[:, k * pair + 128 : k * pair + 256]
                x2 = r[:, k * pair + 256 : k * pair + 384]
                y1 = jnp.where(lane < ROPE, turn(x1, cosine, sine), x1)
                y2 = jnp.where(lane < ROPE, x2, turn(x2, cosine, sine))
                for n, y in enumerate((x0, y1, y2)):
                    to = pl.multiple_of(start + k * pair + n * 128, 128)
                    qbuf[at, pl.ds(to, 128)] = y.astype(BF16)

        @pl.loop(0, 4)
        def _(i):
            width = wukv.shape[1] // 4
            cols = pl.ds(pl.multiple_of(i * width, 128), width)
            r = jnp.dot(lat[at, q_width:], wukv[:, cols], preferred_element_type=F32)
            kvbuf[at, cols] = r.astype(BF16)

    def stores(j):
        at = chip_rows(j)
        return (
            pltpu.make_async_copy(qbuf.at[at], q_out.at[at], out_sem.at[2 * j]),
            pltpu.make_async_copy(kvbuf.at[at], kv_out.at[at], out_sem.at[2 * j + 1]),
        )

    hid_loads[opposite].wait()
    for copy in first_loads:
        copy.wait()
    for copy in late_loads:
        copy.start()
    down(opposite)
    pl.semaphore_wait(barrier, 3)
    pair_copies[opposite].start()
    hid_loads[1].wait()
    down(1)
    pair_copies[1].start()
    pair_copies[opposite].wait_recv()
    for p in range(PIECES):
        for d in range(2):
            ring_put(d, 0, p, chip_sum(opposite, d, p))
            ring_copy(d, 0, p).start()
    hid_loads[3].wait()
    down(3)
    pair_copies[3].start()
    pair_copies[1].wait_recv()
    for p in range(PIECES):
        ring_put(0, 1, p, chip_sum(1, 1, p))
        ring_copy(0, 1, p).start()
    hid_loads[0].wait()
    down(0)
    pair_copies[0].start()
    pair_copies[3].wait_recv()
    for p in range(PIECES):
        ring_put(1, 1, p, chip_sum(3, 0, p))
        ring_copy(1, 1, p).start()
    for copy in late_loads:
        copy.wait()

    for p in range(PIECES):
        for d in range(2):
            ring_copy(d, 0, p).wait_recv()
            ring_put(d, 2, p, chip_sum(toward[d], d, p) + ring_got(d, 0, p))
            ring_copy(d, 2, p).start()

    pair_copies[0].wait_recv()
    for p in range(PIECES):
        for h in range(2):
            ring_copy(1 - h, 1, p).wait_recv()
            ring_copy(h, 2, p).wait_recv()
            total = chip_sum(0, h, p) + ring_got(1 - h, 1, p) + ring_got(h, 2, p)
            q = total[:, :q_width]
            kv = total[:, q_width:latent_width]
            q_scale = lax.rsqrt(jnp.mean(q * q, axis=1, keepdims=True) + 1e-06)
            kv_scale = lax.rsqrt(jnp.mean(kv * kv, axis=1, keepdims=True) + 1e-06)
            at = lat_rows(0, core, h, p)
            lat[at, :q_width] = (q * q_scale * qg[...]).astype(BF16)
            lat[at, q_width:] = (kv * kv_scale * kvg[...]).astype(BF16)
            gather_copy(h, 0, p).start()
            gather_copy(1 - h, 1, p).start()
            forward(0, h, p).start()
            key = total[:, latent_width:]
            first = key[:, : ROPE // 2]
            second = key[:, ROPE // 2 :]
            cosine = tab[0, at, : ROPE // 2]
            sine = tab[1, at, ROPE // 2 : ROPE]
            keybuf[piece_rows(h, p), :] = jnp.concatenate(
                [first * cosine - second * sine, second * cosine + first * sine], axis=1
            ).astype(BF16)
    key_copy = pltpu.make_async_copy(keybuf, key_out, out_sem.at[8])
    key_copy.start()

    forward_wait(0)
    up(0)
    for copy in stores(0):
        copy.start()

    for p in range(PIECES):
        for d in range(2):
            gather_wait(d, 0, p)
            gather_copy(d, 2, p).start()
            forward(behind[d], d, p).start()
        for d in range(2):
            gather_wait(d, 1, p)
            forward(behind[d], 1 - d, p).start()
    for j in (1, 3):
        forward_wait(j)
        up(j)
        for copy in stores(j):
            copy.start()

    for p in range(PIECES):
        for d in range(2):
            gather_wait(d, 2, p)
            forward(opposite, d, p).start()
    forward_wait(opposite)
    up(opposite)
    for copy in stores(opposite):
        copy.start()

    for j in range(CHIPS):
        pair_copies[j].wait_send()
    for d in range(2):
        for stage in range(3):
            for p in range(PIECES):
                ring_copy(d, stage, p).wait_send()
                gather_copy(d, stage, p).wait_send()
    for j in range(CHIPS):
        for h in range(2):
            for p in range(PIECES):
                forward(j, h, p).wait_send()
    key_copy.wait()
    for j in range(CHIPS):
        for copy in stores(j):
            copy.wait()


def shards(hidden, w_dq, w_dkv, q_gain, kv_gain, w_uq, w_ukv):
    rows = hidden.shape[0]
    features, q_width = w_dq.shape
    kv_width = kv_gain.shape[0]
    down_width = q_width + w_dkv.shape[1]
    latent_width = q_width + kv_width
    block = rows // (2 * CHIPS)
    half = block // 2
    table = jnp.asarray(rotary_tables(rows))
    dma = pltpu.SemaphoreType.DMA
    any_spec = pl.BlockSpec(memory_space=pl.ANY)
    flops = 2 * rows * (features * down_width + q_width * w_uq.shape[1] + kv_width * w_ukv.shape[1])
    return pl.pallas_call(
        kernel,
        out_shape=(
            jax.ShapeDtypeStruct((rows, w_uq.shape[1]), BF16),
            jax.ShapeDtypeStruct((rows, w_ukv.shape[1]), BF16),
            jax.ShapeDtypeStruct((block, ROPE), BF16),
        ),
        in_specs=[any_spec] * 8,
        out_specs=(any_spec,) * 3,
        scratch_shapes=[
            pltpu.VMEM(hidden.shape, BF16),
            pltpu.VMEM(w_dq.shape, BF16),
            pltpu.VMEM(w_dkv.shape, BF16),
            pltpu.VMEM((1, q_width), F32),
            pltpu.VMEM((1, kv_width), F32),
            pltpu.VMEM(w_uq.shape, BF16),
            pltpu.VMEM(w_ukv.shape, BF16),
            pltpu.VMEM(table.shape, F32),
            pltpu.VMEM((CHIPS, block, down_width), F32),
            pltpu.VMEM((CHIPS, block, down_width), BF16),
            pltpu.VMEM((CHIPS, block, down_width), BF16),
            pltpu.VMEM((2, 3, half, down_width), BF16),
            pltpu.VMEM((2, 3, half, down_width), BF16),
            pltpu.VMEM((rows, latent_width), BF16),
            pltpu.VMEM((rows, w_uq.shape[1]), BF16),
            pltpu.VMEM((rows, w_ukv.shape[1]), BF16),
            pltpu.VMEM((block, ROPE), BF16),
            dma((11,)),
            dma((CHIPS,)), dma((CHIPS,)),
            dma((2, 3, PIECES)), dma((2, 3, PIECES)),
            dma((2, 3, PIECES)), dma((2, 3, PIECES)),
            dma((CHIPS, 2, PIECES)), dma((CHIPS, 2, PIECES)),
            dma((9,)),
        ],
        compiler_params=pltpu.CompilerParams(
            collective_id=0, has_side_effects=True, vmem_limit_bytes=60 * 1024 * 1024
        ),
        cost_estimate=pl.CostEstimate(flops=flops, bytes_accessed=20_000_000, transcendentals=0),
    )(
        hidden, w_dq, w_dkv, q_gain.reshape(1, -1), kv_gain.reshape(1, -1), w_uq, w_ukv, table
    )


def solution(mesh):
    in_specs = (
        P("dp", "tensor"),
        P("tensor", None),
        P("tensor", None),
        P(),
        P(),
        P(None, "tensor"),
        P(None, "tensor"),
    )
    out_specs = (P("dp", "tensor"), P("dp", "tensor"), P(("dp", "tensor"), None))
    return jax.shard_map(shards, mesh=mesh, in_specs=in_specs, out_specs=out_specs, check_vma=False)
```

time: 219 us -> 104 us (0.47)
  waiting for transfers between devices: 156 us -> 0 us
  Pallas kernels: 0 us -> 91.5 us
  matrix products: 22.5 us -> 0 us
  other arithmetic: 16.4 us -> 0 us
  between operations: 14.1 us -> 0.64 us
  local copies, waits for them, and re-layouts: 6.69 us -> 11 us
    reduce_scatter x1 -> x0, waiting for transfers between devices: 98.7 us -> none  [shards(): lax.psum_scatter(jnp.concatenate([jnp.dot(hidden, w_dq, preferred_element...]
    pallas_call x0 -> x1, Pallas kernels: none -> 91.5 us  [shards(): pl.pallas_call(kernel, out_shape=(jax.ShapeDtypeStruct((rows, w_uq.shape[...]
    all_gather x1 -> x0, waiting for transfers between devices: 57.4 us -> none  [shards(): piece = lax.all_gather(latent, 'tensor', axis=0, tiled=True)]
    dot_general x4 -> x0, matrix products: 22.5 us -> none  [the longest x1 8.14 us: shards(): jnp.dot(piece[:, :q_width], w_uq, preferred_element_type=jnp.float32)]
    concatenate x4 -> x0, other arithmetic: 9.7 us -> none  [the longest x1 6.4 us: shards(): jnp.concatenate([jnp.dot(hidden, w_dq, preferred_element_type=jnp.float32...]
    convert_element_type x4 -> x0, other arithmetic: 2.5 us -> none  [the longest x2 2.48 us: normalize(): return (block * scale * gain[None, :]).astype(jnp.bfloat16)]
    reduce_sum x2 -> x0, other arithmetic: 2.39 us -> none  [normalize(): scale = lax.rsqrt(jnp.mean(block * block, axis=1, keepdims=True) + 1e-06)]
    unnamed x11 -> x5, local copies, waits for them, and re-layouts: 6.37 us -> 8.26 us
  transfers between devices with their start and end apart: 2 -> 0, of which waited for: 2 -> 0; matrix products, arithmetic and copies ran while one was open for 1% -> 0% of each run, Pallas kernels for 0% -> 0%
where the time goes in v1:
time: 104 us; the launch traced here: 103 us
  Pallas kernels  91.5 us (88%)
  local copies, waits for them, and re-layouts  11 us (11%)
    pallas_call x1, Pallas kernels, shards(): pl.pallas_call(kernel, out_shape=(jax.ShapeDtypeStruct((rows, w_uq.shape[...  91.5 us
    unnamed x5, local copies, waits for them, and re-layouts  8.26 us

profile of v1, /device:TPU:43, one launch (start us, length us, event | category | flops | bytes accessed | tf_op | source)
XLA Modules:
  0.0 103.1 jit_solution(6186245583447072774)
XLA Ops:
  0.6 1.3 %reshape.12.q_gain = f32[1,1536]{1,0:T(1,128)} reshape(f32[1536]{0:T(1024)} %param.11) | data formatting | bytes 12288 | tf_op jit(solution)/shard_map/reshape | solution.py:359
  1.9 2.3 %copy.11.w_dkv = bf16[896,576]{1,0:T(8,128)(2,1)} copy(bf16[896,576]{0,1:T(8,128)(2,1)} %param.10) | data formatting | bytes 2064384 | tf_op args[2]
  4.3 91.5 %shard_map.103 = (bf16[1024,1536]{1,0:T(8,128)(2,1)}, bf16[1024,2048]{1,0:T(8,128)(2,1)}, bf16[128,64]{1,0:T(8,128)(2,1)}) custom-call(bf16[1024,896]{1,0:T(8,128)(2,1)} %hidden.1, bf16[896,1536]{1,0:T(8,128)(2,1)} %w_dq.1, bf16[896,576]{1,0:T(8,128)(2,1)} %copy.11.w_dkv, f32[1,1536]{1,0:T(1,128)} %reshape.12.q_gain, f32[1,512]{1,0:T(1,128)} %bitcast.1, ...), custom_call_target="tpu_custom_call" | custom-call | flops 10854858752 | bytes 20000000 | tf_op jit(solution)/shard_map/pallas_call | solution.py:320
  95.7 1.4 %copy.12 = bf16[128,64]{0,1:T(8,128)(2,1)} copy(bf16[128,64]{1,0:T(8,128)(2,1)} %get-tuple-element.5) | data formatting | bytes 32768 | tf_op jit(solution)/shard_map/pallas_call | solution.py:320
  97.2 0.0 copy-start
  97.2 3.9 %copy.15 = bf16[1024,1536]{1,0:T(8,128)(2,1)} copy(bf16[1024,1536]{1,0:T(8,128)(2,1)} %get-tuple-element.9) | data formatting | bytes 6291456
  101.1 0.0 copy-done
  101.1 2.0 %copy.16 = bf16[1024,2048]{1,0:T(8,128)(2,1)} copy(bf16[1024,2048]{1,0:T(8,128)(2,1)S(1)} %copy-done) | data formatting | bytes 8388608
Async XLA Ops:
  97.2 3.9 %copy-start = (bf16[1024,2048]{1,0:T(8,128)(2,1)S(1)}, bf16[1024,2048]{1,0:T(8,128)(2,1)}, u32[]{:S(2)}) copy-start(bf16[1024,2048]{1,0:T(8,128)(2,1)} %get-tuple-element.10) | copy-start | bytes 12582916

commit v2 on v0

v2 whole, which is shorter than its diff:
```python
import jax
import jax.numpy as jnp
import numpy as np
from jax import lax
from jax.experimental import pallas as pl
from jax.experimental.pallas import tpu as pltpu
from jax.sharding import PartitionSpec as P

NOPE = 128
ROPE = 64
CHIPS = 4
PIECES = 4
WINDOW = 3
TILE = 16
LANES = 128
MESH = pl.DeviceIdType.MESH
F32 = jnp.float32
BF16 = jnp.bfloat16


def rotary_tables(count):
    half = ROPE // 2
    freqs = (50000.0 ** (-np.arange(half, dtype=np.float32) / half)).astype(np.float32)
    angle = np.arange(count, dtype=np.float32)[:, None] * freqs[None, :]
    cosine = np.cos(angle.astype(np.float64)).astype(np.float32)
    sine = np.sin(angle.astype(np.float64)).astype(np.float32)
    cosine = np.tile(cosine, (1, 4))
    sine = np.concatenate([-sine, sine, -sine, sine], axis=1)
    return np.stack([cosine, sine])


def lanes():
    return lax.broadcasted_iota(jnp.int32, (1, LANES), 1)


def turn(x, cosine, sine):
    low = lax.rem(lanes(), ROPE) < ROPE // 2
    swapped = jnp.where(low, pltpu.roll(x, LANES - ROPE // 2, 1), pltpu.roll(x, ROPE // 2, 1))
    return x * cosine + swapped * sine


def up_queries(blocks, lat, wuq, tab, put):
    q_width = wuq.shape[0]
    pair = 2 * (NOPE + ROPE)
    steps = wuq.shape[1] // (2 * pair)
    lane = lanes()

    @pl.loop(0, steps)
    def _(i):
        start = pl.multiple_of(i * 2 * pair, LANES)
        x = jnp.concatenate([lat[at, :q_width] for at in blocks], axis=0)
        cosine = jnp.concatenate([tab[0, at, :] for at in blocks], axis=0)
        sine = jnp.concatenate([tab[1, at, :] for at in blocks], axis=0)
        r = jnp.dot(x, wuq[:, pl.ds(start, 2 * pair)], preferred_element_type=F32)
        for k in range(2):
            x0 = r[:, k * pair : k * pair + 128]
            x1 = r[:, k * pair + 128 : k * pair + 256]
            x2 = r[:, k * pair + 256 : k * pair + 384]
            y1 = jnp.where(lane < ROPE, turn(x1, cosine, sine), x1)
            y2 = jnp.where(lane < ROPE, x2, turn(x2, cosine, sine))
            for n, y in enumerate((x0, y1, y2)):
                y = y.astype(BF16)
                row = 0
                for b, at in enumerate(blocks):
                    put(b, pl.multiple_of(start + k * pair + n * LANES, LANES), y[row : row + at.size])
                    row += at.size


def up_keys_values(blocks, lat, wukv, put):
    q_width = lat.shape[1] - wukv.shape[0]
    width = 512

    @pl.loop(0, wukv.shape[1] // width)
    def _(i):
        start = pl.multiple_of(i * width, LANES)
        x = jnp.concatenate([lat[at, q_width:] for at in blocks], axis=0)
        y = jnp.dot(x, wukv[:, pl.ds(start, width)], preferred_element_type=F32).astype(BF16)
        row = 0
        for b, at in enumerate(blocks):
            put(b, start, y[row : row + at.size])
            row += at.size


def place():
    me = lax.axis_index("tensor")
    chip = me // 2
    core = me - 2 * chip
    return me, chip, core


def quarter_blocks(chip, block, offsets, g):
    size = block // 4
    return [
        pl.ds(pl.multiple_of((lax.rem(chip + j, CHIPS) * 2 + c) * block + h * 2 * size + g * size, size), size)
        for j in offsets for c in range(2) for h in range(2)
    ]


def kernel(
    hidden, w_dq, w_dkv, q_gain, kv_gain, w_uq, w_ukv, table,
    qbuf, kvbuf, keybuf, lat, wuq, wukv, tab,
    hid, wdq, wdkv, gain, acc, pair_out, pair_in, ring_out, ring_in, keyrow,
    load_sem, first_s, first_r, pair_s, pair_r, rs_s, rs_r, ag_s, ag_r, fw_s, fw_r,
):
    rows = hid.shape[0]
    q_width = w_uq.shape[0]
    kv_width = w_ukv.shape[0]
    latent_width = q_width + kv_width
    q_tiles, tiles = q_width // LANES, latent_width // LANES
    block = rows // (2 * CHIPS)
    half = block // 2
    row_tiles = block // TILE
    strips = 4
    wide = tiles // strips
    me, chip, core = place()
    partner = me + 1 - 2 * core

    def chip_at(j):
        return lax.rem(chip + j, CHIPS)

    neighbour = (chip_at(1) * 2 + core, chip_at(CHIPS - 1) * 2 + core)
    toward = (1, CHIPS - 1)
    behind = (CHIPS - 1, 1)
    opposite = 2

    def load(i, src, dst):
        return pltpu.make_async_copy(src, dst, load_sem.at[i])

    def chip_rows(j):
        return pl.ds(pl.multiple_of(chip_at(j) * 2 * block, 2 * block), 2 * block)

    width = wide * LANES
    hid_loads = [load(j, hidden.at[chip_rows(j)], hid.at[chip_rows(j)]) for j in range(CHIPS)]
    strip_loads = [load(4 + i, w_dq.at[:, pl.ds(i * width, width)], wdq.at[i]) for i in range(strips - 1)]
    strip_loads.append(load(7, w_dkv, wdkv.at[pl.ds(0, kv_width + ROPE)]))
    late_loads = [
        load(8, q_gain, gain.at[pl.ds(0, q_tiles)]), load(9, kv_gain, gain.at[pl.ds(q_tiles, tiles - q_tiles)]),
        load(10, table, tab), load(11, w_ukv, wukv), load(12, w_uq, wuq),
    ]
    hid_loads[opposite].start()
    for copy in strip_loads:
        copy.start()
    for j in (1, 3, 0):
        hid_loads[j].start()

    barrier = pltpu.get_barrier_semaphore()
    for device in (*neighbour, partner):
        pl.semaphore_signal(barrier, inc=1, device_id={"tensor": device}, device_id_type=MESH)
    wdkv[kv_width + ROPE :, :] = jnp.zeros((ROPE, wdkv.shape[1]), BF16)

    def remote(src, dst, send, recv, device):
        return pltpu.make_async_remote_copy(
            src_ref=src, dst_ref=dst, send_sem=send, recv_sem=recv,
            device_id={"tensor": device}, device_id_type=MESH,
        )

    rotary_at = strips * row_tiles * wide
    lane = lanes()

    def down_strip(j, i, weights, depth):
        base = chip_at(j) * 2 * block
        other = pl.ds(pl.multiple_of(base + (1 - core) * block, block), block)
        own = pl.ds(pl.multiple_of(base + core * block, block), block)
        x = jnp.concatenate([hid[other, :], hid[own, :]], axis=0)
        r = lax.dot_general(x, weights, (((1,), (depth,)), ((), ())), preferred_element_type=F32)
        first = i * row_tiles * wide
        for t in range(row_tiles):
            for c in range(wide):
                cols = slice(c * LANES, (c + 1) * LANES)
                low = t * TILE
                pair_out[j, first + t * wide + c] = r[low : low + TILE, cols].astype(BF16)
                acc[j, first + t * wide + c] = r[block + low : block + low + TILE, cols]

    def down_rotary(j):
        base = chip_at(j) * 2 * block
        other = pl.ds(pl.multiple_of(base + (1 - core) * block, block), block)
        own = pl.ds(pl.multiple_of(base + core * block, block), block)
        x = jnp.concatenate([hid[other, :], hid[own, :]], axis=0)
        r = lax.dot_general(x, wdkv[kv_width:, :], (((1,), (1,)), ((), ())), preferred_element_type=F32)
        for side in range(2):
            for g in range(row_tiles // 2):
                low = side * block + g * 2 * TILE
                a, b = r[low : low + TILE], r[low + TILE : low + 2 * TILE]
                packed = jnp.where(lane < ROPE, a, pltpu.roll(b, ROPE, 1))
                if side == 0:
                    pair_out[j, rotary_at + g] = packed.astype(BF16)
                else:
                    acc[j, rotary_at + g] = packed

    def down_last(j):
        down_strip(j, strips - 1, wdkv[:kv_width, :], 1)
        down_rotary(j)

    def first_copy(i):
        size = row_tiles * wide
        at = pl.ds(i * size, size + (row_tiles // 2 if i == strips - 1 else 0))
        return remote(
            pair_out.at[opposite, at], pair_in.at[opposite, at], first_s.at[i], first_r.at[i], partner
        )

    def pair_copy(j):
        return remote(pair_out.at[j], pair_in.at[j], pair_s.at[j], pair_r.at[j], partner)

    def strip_sum(j, i, t, count):
        at = pl.ds((i * row_tiles + t) * wide, count * wide)
        return acc[j, at] + pair_in[j, at].astype(F32)

    def row_sum(j, t):
        return jnp.concatenate([strip_sum(j, i, t, 1) for i in range(strips)], axis=0)

    def rotary_sum(j, h):
        at = pl.ds(rotary_at + h * 2, 2)
        return acc[j, at] + pair_in[j, at].astype(F32)

    def run(stage, p):
        if stage == 0:
            return pl.ds(p * tiles, tiles + (2 if p == PIECES - 1 else 0))
        return pl.ds(0, tiles + 2) if p == 0 else pl.ds(p * tiles + 2, tiles)

    def run_tiles(stage, p):
        return pl.ds(run(stage, p).start, tiles)

    def rotary_tiles(stage):
        return pl.ds(PIECES * tiles if stage == 0 else tiles, 2)

    def ring_copy(d, stage, p):
        at = run(stage, p)
        return remote(
            ring_out.at[d, stage, at], ring_in.at[d, stage, at],
            rs_s.at[d, stage, p], rs_r.at[d, stage, p], neighbour[d],
        )

    def lat_rows(j, c, h, p):
        start = (chip_at(j) * 2 + c) * block + h * half + p * TILE
        return pl.ds(pl.multiple_of(start, TILE), TILE)

    def gather_copy(d, stage, p):
        j = (0, 0, behind[d])[stage]
        h = (d, 1 - d, d)[stage]
        at = lat.at[lat_rows(j, core, h, p)]
        return remote(at, at, ag_s.at[d, stage, p], ag_r.at[d, stage, p], neighbour[d])

    def gather_wait(d, stage, p):
        j = (behind[d], behind[d], opposite)[stage]
        h = (d, 1 - d, d)[stage]
        at = lat.at[lat_rows(j, core, h, p)]
        remote(at, at, ag_s.at[d, stage, p], ag_r.at[d, stage, p], neighbour[d]).wait_recv()

    def forward(j, h, p):
        at = lat.at[lat_rows(j, core, h, p)]
        return remote(at, at, fw_s.at[j, h, p], fw_r.at[j, h, p], partner)

    def forward_wait(j, p):
        for h in range(2):
            at = lat.at[lat_rows(j, 1 - core, h, p)]
            remote(at, at, fw_s.at[j, h, p], fw_r.at[j, h, p], partner).wait_recv()

    sent = ([], [])

    def send(d, copy):
        if len(sent[d]) >= PIECES:
            sent[d][len(sent[d]) - WINDOW].wait_send()
        copy.start()
        sent[d].append(copy)

    def queries_in(blocks):
        def put(b, column, values):
            qbuf[blocks[b], pl.ds(column, LANES)] = values
        up_queries(blocks, lat, wuq, tab, put)

    def keys_values_in(blocks):
        def put(b, column, values):
            kvbuf[blocks[b], pl.ds(column, 512)] = values
        up_keys_values(blocks, lat, wukv, put)

    def first_send(i):
        first_copy(i).wait_recv()
        for d in range(2):
            t = d * PIECES
            ring_out[d, 0, pl.ds(i * tiles, tiles)] = strip_sum(opposite, i, t, PIECES).astype(BF16)
            if i == strips - 1:
                ring_out[d, 0, rotary_tiles(0)] = rotary_sum(opposite, d).astype(BF16)
            send(d, ring_copy(d, 0, i))

    hid_loads[opposite].wait()
    for i in range(strips):
        strip_loads[i].wait()
        if i < strips - 1:
            down_strip(opposite, i, wdq[i], 0)
        else:
            down_last(opposite)
        if i == 0:
            pl.semaphore_wait(barrier, 3)
        first_copy(i).start()
        if i == 1:
            for copy in late_loads:
                copy.start()
        if i > 0:
            first_send(i - 1)
    first_send(strips - 1)

    for j in (1, 3, 0):
        hid_loads[j].wait()

        @pl.loop(0, strips - 1)
        def _(i):
            down_strip(j, i, wdq[i], 0)

        down_last(j)
        pair_copy(j).start()

    for copy in late_loads:
        copy.wait()

    for d in range(2):
        pair_copy(toward[d]).wait_recv()
    for p in range(PIECES):
        for d in range(2):
            h = 1 - d
            ring_out[d, 1, run_tiles(1, p)] = row_sum(toward[d], h * PIECES + p).astype(BF16)
            if p == 0:
                ring_out[d, 1, rotary_tiles(1)] = rotary_sum(toward[d], h).astype(BF16)
            send(d, ring_copy(d, 1, p))

    for i in range(strips):
        for d in range(2):
            ring_copy(d, 0, i).wait_recv()
    for p in range(PIECES):
        for d in range(2):
            got = jnp.concatenate(
                [ring_in[d, 0, pl.ds(i * tiles + p * wide, wide)] for i in range(strips)], axis=0
            ).astype(F32)
            total = row_sum(toward[d], d * PIECES + p) + got
            ring_out[d, 2, run_tiles(2, p)] = total.astype(BF16)
            if p == 0:
                total = rotary_sum(toward[d], d) + ring_in[d, 0, rotary_tiles(0)].astype(F32)
                ring_out[d, 2, rotary_tiles(2)] = total.astype(BF16)
            send(d, ring_copy(d, 2, p))

    pair_copy(0).wait_recv()
    for p in range(PIECES):
        for h in range(2):
            ring_copy(1 - h, 1, p).wait_recv()
            ring_copy(h, 2, p).wait_recv()
            total = row_sum(0, h * PIECES + p)
            total += ring_in[1 - h, 1, run_tiles(1, p)].astype(F32) + ring_in[h, 2, run_tiles(2, p)].astype(F32)
            at = lat_rows(0, core, h, p)
            for first, end in ((0, q_tiles), (q_tiles, tiles)):
                part = total[first:end]
                squares = jnp.sum(jnp.sum(part * part, axis=0), axis=1, keepdims=True)
                scale = lax.rsqrt(squares / ((end - first) * LANES) + 1e-06)
                for k in range(first, end):
                    value = total[k] * scale * gain[k : k + 1, :]
                    lat[at, k * LANES : (k + 1) * LANES] = value.astype(BF16)
            forward(0, h, p).start()
        for d in range(2):
            send(d, gather_copy(d, 0, p))
        for d in range(2):
            send(d, gather_copy(d, 1, p))
    for h in range(2):
        total = rotary_sum(0, h)
        total += ring_in[1 - h, 1, rotary_tiles(1)].astype(F32) + ring_in[h, 2, rotary_tiles(2)].astype(F32)
        for g in range(2):
            a, b = lat_rows(0, core, h, 2 * g), lat_rows(0, core, h, 2 * g + 1)
            cosine = jnp.where(lane < ROPE, tab[0, a, :], tab[0, b, :])
            sine = jnp.where(lane < ROPE, tab[1, a, :], tab[1, b, :])
            turned = turn(total[g], cosine, sine)
            low = h * half + 2 * g * TILE
            keyrow[low : low + TILE, :] = turned
            keyrow[low + TILE : low + 2 * TILE, :] = pltpu.roll(turned, ROPE, 1)
    keybuf[...] = keyrow[...].T[:ROPE].astype(BF16)

    for p in range(PIECES):
        forward_wait(0, p)
    queries_in([chip_rows(0)])

    for p in range(PIECES):
        for d in range(2):
            gather_wait(d, 0, p)
            forward(behind[d], d, p).start()
            send(d, gather_copy(d, 2, p))
        if p == 0:
            keys_values_in([chip_rows(0)])
        for d in range(2):
            gather_wait(d, 1, p)
            forward(behind[d], 1 - d, p).start()
        if p == 1:
            near = quarter_blocks(chip, block, (1, 3), 0)
            for q in range(2):
                forward_wait(1, q)
                forward_wait(3, q)
            queries_in(near)
    keys_values_in(near)
    near = quarter_blocks(chip, block, (1, 3), 1)
    for q in range(2, PIECES):
        forward_wait(1, q)
        forward_wait(3, q)
    queries_in(near)

    for p in range(PIECES // 2):
        for d in range(2):
            gather_wait(d, 2, p)
            forward(opposite, d, p).start()
    keys_values_in(near)
    for p in range(PIECES // 2):
        forward_wait(opposite, p)
    far = quarter_blocks(chip, block, (opposite,), 0)
    queries_in(far)
    keys_values_in(far)
    for p in range(PIECES // 2, PIECES):
        for d in range(2):
            gather_wait(d, 2, p)
            forward(opposite, d, p).start()

    for i in range(strips):
        first_copy(i).wait_send()
    for j in (1, 3, 0):
        pair_copy(j).wait_send()
    for d in range(2):
        for copy in sent[d][: PIECES - WINDOW] + sent[d][len(sent[d]) - WINDOW :]:
            copy.wait_send()
    for j in range(CHIPS):
        for h in range(2):
            for p in range(PIECES):
                forward(j, h, p).wait_send()
    for p in range(PIECES // 2, PIECES):
        forward_wait(opposite, p)


def store(q, kv, key, lat, wuq, wukv, tab, q_out, kv_out, key_out, qlast, kvlast, sem, last_sem):
    _, chip, _ = place()
    block = q.shape[0] // (2 * CHIPS)
    last = quarter_blocks(chip, block, (2,), 1)
    copies = [pltpu.make_async_copy(key, key_out, sem.at[0])]

    def add(at):
        for src, dst in ((q, q_out), (kv, kv_out)):
            copies.append(pltpu.make_async_copy(src.at[at], dst.at[at], sem.at[len(copies)]))

    for j in (0, 1, 3):
        add(pl.ds(pl.multiple_of(lax.rem(chip + j, CHIPS) * 2 * block, 2 * block), 2 * block))
    for at in quarter_blocks(chip, block, (2,), 0):
        add(at)
    for copy in copies:
        copy.start()

    def put_q(b, column, values):
        qlast[b * (block // 4) : (b + 1) * (block // 4), pl.ds(column, LANES)] = values

    def put_kv(b, column, values):
        kvlast[b * (block // 4) : (b + 1) * (block // 4), pl.ds(column, 512)] = values

    def finish(n, src, dst):
        made = [
            pltpu.make_async_copy(src.at[pl.ds(b * (block // 4), block // 4)], dst.at[at], last_sem.at[n, b])
            for b, at in enumerate(last)
        ]
        for copy in made:
            copy.start()
        copies.extend(made)

    up_keys_values(last, lat, wukv, put_kv)
    finish(0, kvlast, kv_out)
    up_queries(last, lat, wuq, tab, put_q)
    finish(1, qlast, q_out)
    for copy in copies:
        copy.wait()


def shards(hidden, w_dq, w_dkv, q_gain, kv_gain, w_uq, w_ukv):
    rows = hidden.shape[0]
    features, q_width = w_dq.shape
    w_dkv = w_dkv.T
    kv_width = kv_gain.shape[0]
    tiles = (q_width + kv_width) // LANES
    block = rows // (2 * CHIPS)
    table = jnp.asarray(rotary_tables(rows))
    dma = pltpu.SemaphoreType.DMA
    any_spec = pl.BlockSpec(memory_space=pl.ANY)
    vmem_spec = pl.BlockSpec(memory_space=pltpu.VMEM)
    shapes = ((rows, w_uq.shape[1]), (rows, w_ukv.shape[1]), (ROPE, block))
    flops = 2 * rows * (features * (q_width + w_dkv.shape[0]) + q_width * w_uq.shape[1] + kv_width * w_ukv.shape[1])
    pair_tiles = (block // TILE) * tiles + block // TILE // 2
    results = pl.pallas_call(
        kernel,
        out_shape=(
            *(pltpu.VMEM(shape, BF16) for shape in shapes),
            pltpu.VMEM((rows, q_width + kv_width), BF16),
            pltpu.VMEM(w_uq.shape, BF16),
            pltpu.VMEM(w_ukv.shape, BF16),
            pltpu.VMEM(table.shape, F32),
        ),
        in_specs=[any_spec] * 8,
        out_specs=(vmem_spec,) * 7,
        scratch_shapes=[
            pltpu.VMEM(hidden.shape, BF16),
            pltpu.VMEM((3, features, q_width // 3), BF16),
            pltpu.VMEM((kv_width + 2 * ROPE, features), BF16),
            pltpu.VMEM((tiles, LANES), F32),
            pltpu.VMEM((CHIPS, pair_tiles, TILE, LANES), F32),
            pltpu.VMEM((CHIPS, pair_tiles, TILE, LANES), BF16),
            pltpu.VMEM((CHIPS, pair_tiles, TILE, LANES), BF16),
            pltpu.VMEM((2, 3, PIECES * tiles + 2, TILE, LANES), BF16),
            pltpu.VMEM((2, 3, PIECES * tiles + 2, TILE, LANES), BF16),
            pltpu.VMEM((block, LANES), F32),
            dma((13,)),
            dma((4,)), dma((4,)),
            dma((CHIPS,)), dma((CHIPS,)),
            dma((2, 3, PIECES)), dma((2, 3, PIECES)),
            dma((2, 3, PIECES)), dma((2, 3, PIECES)),
            dma((CHIPS, 2, PIECES)), dma((CHIPS, 2, PIECES)),
        ],
        compiler_params=pltpu.CompilerParams(
            collective_id=0, has_side_effects=True, vmem_limit_bytes=47_000_000
        ),
        cost_estimate=pl.CostEstimate(flops=flops, bytes_accessed=13_000_000, transcendentals=0),
    )(
        hidden, w_dq, w_dkv, q_gain.reshape(-1, LANES), kv_gain.reshape(-1, LANES), w_uq, w_ukv, table
    )
    queries, keys_values, rotary = pl.pallas_call(
        store,
        out_shape=tuple(jax.ShapeDtypeStruct(shape, BF16) for shape in shapes),
        in_specs=[vmem_spec] * 7,
        out_specs=(any_spec,) * 3,
        scratch_shapes=[
            pltpu.VMEM((block, w_uq.shape[1]), BF16),
            pltpu.VMEM((block, w_ukv.shape[1]), BF16),
            dma((15,)),
            dma((2, 4)),
        ],
        compiler_params=pltpu.CompilerParams(vmem_limit_bytes=8 * 1024 * 1024),
        cost_estimate=pl.CostEstimate(flops=flops // 16, bytes_accessed=7_400_000, transcendentals=0),
    )(*results)
    return queries, keys_values, rotary.T


def solution(mesh):
    in_specs = (
        P("dp", "tensor"),
        P("tensor", None),
        P("tensor", None),
        P(),
        P(),
        P(None, "tensor"),
        P(None, "tensor"),
    )
    out_specs = (P("dp", "tensor"), P("dp", "tensor"), P(("dp", "tensor"), None))
    return jax.shard_map(shards, mesh=mesh, in_specs=in_specs, out_specs=out_specs, check_vma=False)
```

time: 219 us -> 88 us (0.40); the launches traced: 216 us -> 87.9 us
  waiting for transfers between devices: 156 us -> 0 us
  Pallas kernels: 0 us -> 87.3 us
  matrix products: 22.5 us -> 0 us
  other arithmetic: 16.4 us -> 0 us
  between operations: 14.1 us -> 0.64 us
  local copies, waits for them, and re-layouts: 6.69 us -> 0 us
    reduce_scatter x1 -> x0, waiting for transfers between devices: 98.7 us -> none  [shards(): lax.psum_scatter(jnp.concatenate([jnp.dot(hidden, w_dq, preferred_element...]
    pallas_call x0 -> x2, Pallas kernels: none -> 87.3 us  [the longest x1 84 us: shards(): pl.pallas_call(kernel, out_shape=(*(pltpu.VMEM(shape, BF16) for shape in...]
    all_gather x1 -> x0, waiting for transfers between devices: 57.4 us -> none  [shards(): piece = lax.all_gather(latent, 'tensor', axis=0, tiled=True)]
    dot_general x4 -> x0, matrix products: 22.5 us -> none  [the longest x1 8.14 us: shards(): jnp.dot(piece[:, :q_width], w_uq, preferred_element_type=jnp.float32)]
    concatenate x4 -> x0, other arithmetic: 9.7 us -> none  [the longest x1 6.4 us: shards(): jnp.concatenate([jnp.dot(hidden, w_dq, preferred_element_type=jnp.float32...]
    unnamed x11 -> x0, local copies, waits for them, and re-layouts: 6.37 us -> none
    convert_element_type x4 -> x0, other arithmetic: 2.5 us -> none  [the longest x2 2.48 us: normalize(): return (block * scale * gain[None, :]).astype(jnp.bfloat16)]
    reduce_sum x2 -> x0, other arithmetic: 2.39 us -> none  [normalize(): scale = lax.rsqrt(jnp.mean(block * block, axis=1, keepdims=True) + 1e-06)]
  transfers between devices with their start and end apart: 2 -> 0, of which waited for: 2 -> 0; matrix products, arithmetic and copies ran while one was open for 1% -> 0% of each run, Pallas kernels for 0% -> 0%
where the time goes in v2:
time: 88 us; the launch traced here: 87.9 us
  Pallas kernels  87.3 us (99%)
    pallas_call x1, Pallas kernels, shards(): pl.pallas_call(kernel, out_shape=(*(pltpu.VMEM(shape, BF16) for shape in...  84 us
    pallas_call x1, Pallas kernels, shards(): pl.pallas_call(store, out_shape=tuple((jax.ShapeDtypeStruct(shape, BF16)...  3.22 us

profile of v2, /device:TPU:43, one launch (start us, length us, event | category | flops | bytes accessed | tf_op | source)
XLA Modules:
  0.0 87.9 jit_solution(16035358442229503281)
XLA Ops:
  0.6 84.0 %shard_map.103 = (bf16[1024,1536]{1,0:T(8,128)(2,1)S(1)}, bf16[1024,2048]{1,0:T(8,128)(2,1)S(1)}, bf16[64,128]{1,0:T(8,128)(2,1)S(1)}, bf16[1024,2048]{1,0:T(8,1...) custom-call(bf16[1024,896]{1,0:T(8,128)(2,1)} %hidden.1, ...), custom_call_target="tpu_custom_call" | custom-call | flops 10854858752 | bytes 13000000 | tf_op jit(solution)/shard_map/pallas_call | solution.py:484
  84.7 3.2 %shard_map.104 = (bf16[1024,1536]{1,0:T(8,128)(2,1)}, bf16[1024,2048]{1,0:T(8,128)(2,1)}, bf16[64,128]{1,0:T(8,128)(2,1)}) custom-call(bf16[1024,1536]{1,0:T(8,128)(2,1)S(1)} %get-tuple-element.13.q, bf16[1024,2048]{1,0:T(8,128)(2,1)S(1)} %get-tuple-element.14.kv, bf16[64,128]{1,0:T(8,128)(2,1)S(1)} %get-tuple-element.15.key, ...), custom_call_target="tpu_custom_call" | custom-call | flops 678428672 | bytes 7400000 | tf_op jit(solution)/shard_map/pallas_call | solution.py:520

commit v3 on v2

--- a/solution.py
+++ b/solution.py
@@ -39,20 +39,20 @@
     return x * cosine + swapped * sine
 
 
-def up_queries(blocks, lat, wuq, tab, put):
+def up_queries(blocks, lat, wuq, tab, put, steps):
     q_width = wuq.shape[0]
     pair = 2 * (NOPE + ROPE)
-    steps = wuq.shape[1] // (2 * pair)
+    heads = wuq.shape[1] // (steps * pair)
     lane = lanes()
 
     @pl.loop(0, steps)
     def _(i):
-        start = pl.multiple_of(i * 2 * pair, LANES)
+        start = pl.multiple_of(i * heads * pair, LANES)
         x = jnp.concatenate([lat[at, :q_width] for at in blocks], axis=0)
         cosine = jnp.concatenate([tab[0, at, :] for at in blocks], axis=0)
         sine = jnp.concatenate([tab[1, at, :] for at in blocks], axis=0)
-        r = jnp.dot(x, wuq[:, pl.ds(start, 2 * pair)], preferred_element_type=F32)
-        for k in range(2):
+        r = jnp.dot(x, wuq[:, pl.ds(start, heads * pair)], preferred_element_type=F32)
+        for k in range(heads):
             x0 = r[:, k * pair : k * pair + 128]
             x1 = r[:, k * pair + 128 : k * pair + 256]
             x2 = r[:, k * pair + 256 : k * pair + 384]
@@ -66,11 +66,11 @@
                     row += at.size
 
 
-def up_keys_values(blocks, lat, wukv, put):
+def up_keys_values(blocks, lat, wukv, put, steps):
     q_width = lat.shape[1] - wukv.shape[0]
-    width = 512
-
-    @pl.loop(0, wukv.shape[1] // width)
+    width = wukv.shape[1] // steps
+
+    @pl.loop(0, steps)
     def _(i):
         start = pl.multiple_of(i * width, LANES)
         x = jnp.concatenate([lat[at, q_width:] for at in blocks], axis=0)
@@ -88,10 +88,10 @@
     return me, chip, core
 
 
-def quarter_blocks(chip, block, offsets, g):
-    size = block // 4
+def piece_blocks(chip, block, offsets, first, count):
+    size = count * TILE
     return [
-        pl.ds(pl.multiple_of((lax.rem(chip + j, CHIPS) * 2 + c) * block + h * 2 * size + g * size, size), size)
+        pl.ds(pl.multiple_of((lax.rem(chip + j, CHIPS) * 2 + c) * block + h * (block // 2) + first * TILE, TILE), size)
         for j in offsets for c in range(2) for h in range(2)
     ]
 
@@ -100,7 +100,7 @@
     hidden, w_dq, w_dkv, q_gain, kv_gain, w_uq, w_ukv, table,
     qbuf, kvbuf, keybuf, lat, wuq, wukv, tab,
     hid, wdq, wdkv, gain, acc, pair_out, pair_in, ring_out, ring_in, keyrow,
-    load_sem, first_s, first_r, pair_s, pair_r, rs_s, rs_r, ag_s, ag_r, fw_s, fw_r,
+    load_sem, first_r, pair_s, pair_r, ring_s, rs_first_r, rs_r, ag_r, fw_s, fw_r,
 ):
     rows = hid.shape[0]
     q_width = w_uq.shape[0]
@@ -195,11 +195,11 @@
         size = row_tiles * wide
         at = pl.ds(i * size, size + (row_tiles // 2 if i == strips - 1 else 0))
         return remote(
-            pair_out.at[opposite, at], pair_in.at[opposite, at], first_s.at[i], first_r.at[i], partner
+            pair_out.at[opposite, at], pair_in.at[opposite, at], pair_s.at[0], first_r.at[i], partner
         )
 
     def pair_copy(j):
-        return remote(pair_out.at[j], pair_in.at[j], pair_s.at[j], pair_r.at[j], partner)
+        return remote(pair_out.at[j], pair_in.at[j], pair_s.at[0], pair_r.at[j], partner)
 
     def strip_sum(j, i, t, count):
         at = pl.ds((i * row_tiles + t) * wide, count * wide)
@@ -223,55 +223,68 @@
     def rotary_tiles(stage):
         return pl.ds(PIECES * tiles if stage == 0 else tiles, 2)
 
-    def ring_copy(d, stage, p):
+    def ring_copy(d, stage, p, n=0):
         at = run(stage, p)
+        recv = rs_first_r.at[d] if stage == 0 else rs_r.at[d, stage - 1, p]
         return remote(
-            ring_out.at[d, stage, at], ring_in.at[d, stage, at],
-            rs_s.at[d, stage, p], rs_r.at[d, stage, p], neighbour[d],
+            ring_out.at[d, stage, at], ring_in.at[d, stage, at], ring_s.at[d, n % PIECES], recv, neighbour[d]
         )
+
+    def ring_first_wait(d):
+        remote(
+            ring_out.at[d, 0], ring_in.at[d, 0], ring_s.at[d, 0], rs_first_r.at[d], neighbour[d]
+        ).wait_recv()
 
     def lat_rows(j, c, h, p):
         start = (chip_at(j) * 2 + c) * block + h * half + p * TILE
         return pl.ds(pl.multiple_of(start, TILE), TILE)
 
-    def gather_copy(d, stage, p):
+    def gather_copy(d, stage, p, n):
         j = (0, 0, behind[d])[stage]
         h = (d, 1 - d, d)[stage]
         at = lat.at[lat_rows(j, core, h, p)]
-        return remote(at, at, ag_s.at[d, stage, p], ag_r.at[d, stage, p], neighbour[d])
+        return remote(at, at, ring_s.at[d, n % PIECES], ag_r.at[d, stage, p], neighbour[d])
 
     def gather_wait(d, stage, p):
         j = (behind[d], behind[d], opposite)[stage]
         h = (d, 1 - d, d)[stage]
         at = lat.at[lat_rows(j, core, h, p)]
-        remote(at, at, ag_s.at[d, stage, p], ag_r.at[d, stage, p], neighbour[d]).wait_recv()
+        remote(at, at, ring_s.at[d, 0], ag_r.at[d, stage, p], neighbour[d]).wait_recv()
 
     def forward(j, h, p):
         at = lat.at[lat_rows(j, core, h, p)]
-        return remote(at, at, fw_s.at[j, h, p], fw_r.at[j, h, p], partner)
+        return remote(at, at, fw_s.at[0], fw_r.at[j, p], partner)
 
     def forward_wait(j, p):
-        for h in range(2):
-            at = lat.at[lat_rows(j, 1 - core, h, p)]
-            remote(at, at, fw_s.at[j, h, p], fw_r.at[j, h, p], partner).wait_recv()
+        at = lat.at[pl.ds(0, 2 * TILE)]
+        remote(at, at, fw_s.at[0], fw_r.at[j, p], partner).wait_recv()
 
     sent = ([], [])
 
-    def send(d, copy):
-        if len(sent[d]) >= PIECES:
-            sent[d][len(sent[d]) - WINDOW].wait_send()
+    done = [0, 0]
+
+    def drain(d, end):
+        for copy in sent[d][done[d] : end]:
+            copy.wait_send()
+        done[d] = end
+
+    def send(d, make, *which):
+        n = len(sent[d])
+        if n >= PIECES:
+            drain(d, n - WINDOW + 1)
+        copy = make(d, *which, n)
         copy.start()
         sent[d].append(copy)
 
     def queries_in(blocks):
         def put(b, column, values):
             qbuf[blocks[b], pl.ds(column, LANES)] = values
-        up_queries(blocks, lat, wuq, tab, put)
+        up_queries(blocks, lat, wuq, tab, put, 1)
 
     def keys_values_in(blocks):
         def put(b, column, values):
-            kvbuf[blocks[b], pl.ds(column, 512)] = values
-        up_keys_values(blocks, lat, wukv, put)
+            kvbuf[blocks[b], pl.ds(column, values.shape[1])] = values
+        up_keys_values(blocks, lat, wukv, put, 1)
 
     def first_send(i):
         first_copy(i).wait_recv()
@@ -280,7 +293,7 @@
             ring_out[d, 0, pl.ds(i * tiles, tiles)] = strip_sum(opposite, i, t, PIECES).astype(BF16)
             if i == strips - 1:
                 ring_out[d, 0, rotary_tiles(0)] = rotary_sum(opposite, d).astype(BF16)
-            send(d, ring_copy(d, 0, i))
+            send(d, ring_copy, 0, i)
 
     hid_loads[opposite].wait()
     for i in range(strips):
@@ -320,11 +333,10 @@
             ring_out[d, 1, run_tiles(1, p)] = row_sum(toward[d], h * PIECES + p).astype(BF16)
             if p == 0:
                 ring_out[d, 1, rotary_tiles(1)] = rotary_sum(toward[d], h).astype(BF16)
-            send(d, ring_copy(d, 1, p))
-
-    for i in range(strips):
-        for d in range(2):
-            ring_copy(d, 0, i).wait_recv()
+            send(d, ring_copy, 1, p)
+
+    for d in range(2):
+        ring_first_wait(d)
     for p in range(PIECES):
         for d in range(2):
             got = jnp.concatenate(
@@ -335,10 +347,9 @@
             if p == 0:
                 total = rotary_sum(toward[d], d) + ring_in[d, 0, rotary_tiles(0)].astype(F32)
                 ring_out[d, 2, rotary_tiles(2)] = total.astype(BF16)
-            send(d, ring_copy(d, 2, p))
-
-    pair_copy(0).wait_recv()
-    for p in range(PIECES):
+            send(d, ring_copy, 2, p)
+
+    def totals(p):
         for h in range(2):
             ring_copy(1 - h, 1, p).wait_recv()
             ring_copy(h, 2, p).wait_recv()
@@ -353,10 +364,54 @@
                     value = total[k] * scale * gain[k : k + 1, :]
                     lat[at, k * LANES : (k + 1) * LANES] = value.astype(BF16)
             forward(0, h, p).start()
+
+    def sends(stage, p):
         for d in range(2):
-            send(d, gather_copy(d, 0, p))
+            send(d, gather_copy, stage, p)
+
+    def near(stage, p):
         for d in range(2):
-            send(d, gather_copy(d, 1, p))
+            gather_wait(d, stage, p)
+            forward(behind[d], (d, 1 - d)[stage], p).start()
+
+    def far(p):
+        for d in range(2):
+            gather_wait(d, 2, p)
+            forward(opposite, d, p).start()
+
+    def ready(offsets, first, count):
+        for p in range(first, first + count):
+            for j in offsets:
+                forward_wait(j, p)
+        return piece_blocks(chip, block, offsets, first, count)
+
+    pair_copy(0).wait_recv()
+    totals(0)
+    sends(0, 0)
+    totals(1)
+    sends(1, 0)
+    totals(2)
+    own = ready((0,), 0, 2)
+    queries_in(own)
+    keys_values_in(own)
+    sends(0, 1)
+    totals(3)
+    sends(1, 1)
+    own = ready((0,), 2, 2)
+    queries_in(own)
+    keys_values_in(own)
+    sends(0, 2)
+    near(0, 0)
+    sends(1, 2)
+    near(1, 0)
+    sends(0, 3)
+    near(0, 1)
+    sends(1, 3)
+    near(1, 1)
+    near_rows = ready((1, 3), 0, 2)
+    queries_in(near_rows)
+    sends(2, 0)
+    keys_values_in(near_rows)
     for h in range(2):
         total = rotary_sum(0, h)
         total += ring_in[1 - h, 1, rotary_tiles(1)].astype(F32) + ring_in[h, 2, rotary_tiles(2)].astype(F32)
@@ -369,102 +424,65 @@
             keyrow[low : low + TILE, :] = turned
             keyrow[low + TILE : low + 2 * TILE, :] = pltpu.roll(turned, ROPE, 1)
     keybuf[...] = keyrow[...].T[:ROPE].astype(BF16)
-
-    for p in range(PIECES):
-        forward_wait(0, p)
-    queries_in([chip_rows(0)])
-
-    for p in range(PIECES):
-        for d in range(2):
-            gather_wait(d, 0, p)
-            forward(behind[d], d, p).start()
-            send(d, gather_copy(d, 2, p))
-        if p == 0:
-            keys_values_in([chip_rows(0)])
-        for d in range(2):
-            gather_wait(d, 1, p)
-            forward(behind[d], 1 - d, p).start()
-        if p == 1:
-            near = quarter_blocks(chip, block, (1, 3), 0)
-            for q in range(2):
-                forward_wait(1, q)
-                forward_wait(3, q)
-            queries_in(near)
-    keys_values_in(near)
-    near = quarter_blocks(chip, block, (1, 3), 1)
-    for q in range(2, PIECES):
-        forward_wait(1, q)
-        forward_wait(3, q)
-    queries_in(near)
-
-    for p in range(PIECES // 2):
-        for d in range(2):
-            gather_wait(d, 2, p)
-            forward(opposite, d, p).start()
-    keys_values_in(near)
-    for p in range(PIECES // 2):
-        forward_wait(opposite, p)
-    far = quarter_blocks(chip, block, (opposite,), 0)
-    queries_in(far)
-    keys_values_in(far)
-    for p in range(PIECES // 2, PIECES):
-        for d in range(2):
-            gather_wait(d, 2, p)
-            forward(opposite, d, p).start()
-
-    for i in range(strips):
-        first_copy(i).wait_send()
-    for j in (1, 3, 0):
-        pair_copy(j).wait_send()
+    sends(2, 1)
+    near(0, 2)
+    sends(2, 2)
+    near(1, 2)
+    near(0, 3)
+    sends(2, 3)
+    near_rows = ready((1, 3), 2, 1)
+    queries_in(near_rows)
+    keys_values_in(near_rows)
+    near(1, 3)
+    far(0)
+    near_rows = ready((1, 3), 3, 1)
+    queries_in(near_rows)
+    far(1)
+    keys_values_in(near_rows)
+    far(2)
+    far_rows = ready((opposite,), 0, 2)
+    queries_in(far_rows)
+    far(3)
+    keys_values_in(far_rows)
+
+    remote(pair_out, pair_in, pair_s.at[0], pair_r.at[0], partner).wait_send()
     for d in range(2):
-        for copy in sent[d][: PIECES - WINDOW] + sent[d][len(sent[d]) - WINDOW :]:
-            copy.wait_send()
-    for j in range(CHIPS):
-        for h in range(2):
-            for p in range(PIECES):
-                forward(j, h, p).wait_send()
+        drain(d, len(sent[d]))
+    whole = lat.at[pl.ds(0, CHIPS * block)]
+    remote(whole, whole, fw_s.at[0], fw_r.at[0, 0], partner).wait_send()
     for p in range(PIECES // 2, PIECES):
         forward_wait(opposite, p)
 
 
-def store(q, kv, key, lat, wuq, wukv, tab, q_out, kv_out, key_out, qlast, kvlast, sem, last_sem):
+def store(q, kv, key, lat, wuq, wukv, tab, q_out, kv_out, key_out, qlast, kvlast, sem):
     _, chip, _ = place()
     block = q.shape[0] // (2 * CHIPS)
-    last = quarter_blocks(chip, block, (2,), 1)
-    copies = [pltpu.make_async_copy(key, key_out, sem.at[0])]
-
-    def add(at):
-        for src, dst in ((q, q_out), (kv, kv_out)):
-            copies.append(pltpu.make_async_copy(src.at[at], dst.at[at], sem.at[len(copies)]))
-
-    for j in (0, 1, 3):
-        add(pl.ds(pl.multiple_of(lax.rem(chip + j, CHIPS) * 2 * block, 2 * block), 2 * block))
-    for at in quarter_blocks(chip, block, (2,), 0):
-        add(at)
-    for copy in copies:
-        copy.start()
+    last = piece_blocks(chip, block, (2,), 2, 2)
+    pltpu.make_async_copy(key, key_out, sem.at[2]).start()
+    early = [
+        pl.ds(pl.multiple_of(lax.rem(chip + j, CHIPS) * 2 * block, 2 * block), 2 * block) for j in (0, 1, 3)
+    ]
+    for at in early + piece_blocks(chip, block, (2,), 0, 2):
+        pltpu.make_async_copy(q.at[at], q_out.at[at], sem.at[0]).start()
+        pltpu.make_async_copy(kv.at[at], kv_out.at[at], sem.at[1]).start()
 
     def put_q(b, column, values):
         qlast[b * (block // 4) : (b + 1) * (block // 4), pl.ds(column, LANES)] = values
 
     def put_kv(b, column, values):
-        kvlast[b * (block // 4) : (b + 1) * (block // 4), pl.ds(column, 512)] = values
-
-    def finish(n, src, dst):
-        made = [
-            pltpu.make_async_copy(src.at[pl.ds(b * (block // 4), block // 4)], dst.at[at], last_sem.at[n, b])
-            for b, at in enumerate(last)
-        ]
-        for copy in made:
-            copy.start()
-        copies.extend(made)
-
-    up_keys_values(last, lat, wukv, put_kv)
-    finish(0, kvlast, kv_out)
-    up_queries(last, lat, wuq, tab, put_q)
-    finish(1, qlast, q_out)
-    for copy in copies:
-        copy.wait()
+        kvlast[b * (block // 4) : (b + 1) * (block // 4), pl.ds(column, values.shape[1])] = values
+
+    def finish(src, dst, done):
+        for b, at in enumerate(last):
+            pltpu.make_async_copy(src.at[pl.ds(b * (block // 4), block // 4)], dst.at[at], done).start()
+
+    up_keys_values(last, lat, wukv, put_kv, 2)
+    finish(kvlast, kv_out, sem.at[1])
+    up_queries(last, lat, wuq, tab, put_q, 2)
+    finish(qlast, q_out, sem.at[0])
+    pltpu.make_async_copy(q, q_out, sem.at[0]).wait()
+    pltpu.make_async_copy(kv, kv_out, sem.at[1]).wait()
+    pltpu.make_async_copy(key, key_out, sem.at[2]).wait()
 
 
 def shards(hidden, w_dq, w_dkv, q_gain, kv_gain, w_uq, w_ukv):
@@ -504,11 +522,9 @@
             pltpu.VMEM((2, 3, PIECES * tiles + 2, TILE, LANES), BF16),
             pltpu.VMEM((block, LANES), F32),
             dma((13,)),
-            dma((4,)), dma((4,)),
-            dma((CHIPS,)), dma((CHIPS,)),
-            dma((2, 3, PIECES)), dma((2, 3, PIECES)),
-            dma((2, 3, PIECES)), dma((2, 3, PIECES)),
-            dma((CHIPS, 2, PIECES)), dma((CHIPS, 2, PIECES)),
+            dma((4,)), dma((1,)), dma((CHIPS,)),
+            dma((2, PIECES)), dma((2,)), dma((2, 2, PIECES)), dma((2, 3, PIECES)),
+            dma((1,)), dma((CHIPS, PIECES)),
         ],
         compiler_params=pltpu.CompilerParams(
             collective_id=0, has_side_effects=True, vmem_limit_bytes=47_000_000
@@ -525,8 +541,7 @@
         scratch_shapes=[
             pltpu.VMEM((block, w_uq.shape[1]), BF16),
             pltpu.VMEM((block, w_ukv.shape[1]), BF16),
-            dma((15,)),
-            dma((2, 4)),
+            dma((3,)),
         ],
         compiler_params=pltpu.CompilerParams(vmem_limit_bytes=8 * 1024 * 1024),
         cost_estimate=pl.CostEstimate(flops=flops // 16, bytes_accessed=7_400_000, transcendentals=0),

time: 88 us -> 84.8 us (0.964)
  Pallas kernels: 87.3 us -> 84.1 us
    pallas_call x1, Pallas kernels: 84 us -> 81.1 us  [shards(): pl.pallas_call(kernel, out_shape=(*(pltpu.VMEM(shape, BF16) for shape in...]
where the time goes in v3:
time: 84.8 us; the launch traced here: 84.7 us
  Pallas kernels  84.1 us (99%)
    pallas_call x1, Pallas kernels, shards(): pl.pallas_call(kernel, out_shape=(*(pltpu.VMEM(shape, BF16) for shape in...  81.1 us
    pallas_call x1, Pallas kernels, shards(): pl.pallas_call(store, out_shape=tuple((jax.ShapeDtypeStruct(shape, BF16)...  2.99 us

profile of v3, /device:TPU:43, one launch (start us, length us, event | category | flops | bytes accessed | tf_op | source)
XLA Modules:
  0.0 84.7 jit_solution(13719810593939501301)
XLA Ops:
  0.6 81.1 %shard_map.103 = (bf16[1024,1536]{1,0:T(8,128)(2,1)S(1)}, bf16[1024,2048]{1,0:T(8,128)(2,1)S(1)}, bf16[64,128]{1,0:T(8,128)(2,1)S(1)}, bf16[1024,2048]{1,0:T(8,1...) custom-call(bf16[1024,896]{1,0:T(8,128)(2,1)} %hidden.1, ...), custom_call_target="tpu_custom_call" | custom-call | flops 10854858752 | bytes 13000000 | tf_op jit(solution)/shard_map/pallas_call | solution.py:502
  81.7 3.0 %shard_map.104 = (bf16[1024,1536]{1,0:T(8,128)(2,1)}, bf16[1024,2048]{1,0:T(8,128)(2,1)}, bf16[64,128]{1,0:T(8,128)(2,1)}) custom-call(bf16[1024,1536]{1,0:T(8,128)(2,1)S(1)} %get-tuple-element.13.q, bf16[1024,2048]{1,0:T(8,128)(2,1)S(1)} %get-tuple-element.14.kv, bf16[64,128]{1,0:T(8,128)(2,1)S(1)} %get-tuple-element.15.key, ...), custom_call_target="tpu_custom_call" | custom-call | flops 678428672 | bytes 7400000 | tf_op jit(solution)/shard_map/pallas_call | solution.py:536

commit v4 on v3

--- a/solution.py
+++ b/solution.py
@@ -10,7 +10,7 @@
 ROPE = 64
 CHIPS = 4
 PIECES = 4
-WINDOW = 3
+WINDOWS = (2, 3)
 TILE = 16
 LANES = 128
 MESH = pl.DeviceIdType.MESH
@@ -137,15 +137,12 @@
         load(8, q_gain, gain.at[pl.ds(0, q_tiles)]), load(9, kv_gain, gain.at[pl.ds(q_tiles, tiles - q_tiles)]),
         load(10, table, tab), load(11, w_ukv, wukv), load(12, w_uq, wuq),
     ]
-    hid_loads[opposite].start()
-    for copy in strip_loads:
-        copy.start()
-    for j in (1, 3, 0):
-        hid_loads[j].start()
-
     barrier = pltpu.get_barrier_semaphore()
     for device in (*neighbour, partner):
         pl.semaphore_signal(barrier, inc=1, device_id={"tensor": device}, device_id_type=MESH)
+    hid_loads[opposite].start()
+    for copy in strip_loads[:2]:
+        copy.start()
     wdkv[kv_width + ROPE :, :] = jnp.zeros((ROPE, wdkv.shape[1]), BF16)
 
     def remote(src, dst, send, recv, device):
@@ -199,7 +196,7 @@
         )
 
     def pair_copy(j):
-        return remote(pair_out.at[j], pair_in.at[j], pair_s.at[0], pair_r.at[j], partner)
+        return remote(pair_out.at[j], pair_in.at[j], pair_s.at[0], pair_r.at[0 if j == 0 else 1], partner)
 
     def strip_sum(j, i, t, count):
         at = pl.ds((i * row_tiles + t) * wide, count * wide)
@@ -225,15 +222,14 @@
 
     def ring_copy(d, stage, p, n=0):
         at = run(stage, p)
-        recv = rs_first_r.at[d] if stage == 0 else rs_r.at[d, stage - 1, p]
+        recv = rs_first_r.at[0] if stage == 0 else rs_r.at[p]
         return remote(
             ring_out.at[d, stage, at], ring_in.at[d, stage, at], ring_s.at[d, n % PIECES], recv, neighbour[d]
         )
 
-    def ring_first_wait(d):
-        remote(
-            ring_out.at[d, 0], ring_in.at[d, 0], ring_s.at[d, 0], rs_first_r.at[d], neighbour[d]
-        ).wait_recv()
+    def tiles_wait(count, recv):
+        at = pair_in.at[0, pl.ds(0, count)]
+        remote(at, at, pair_s.at[0], recv, partner).wait_recv()
 
     def lat_rows(j, c, h, p):
         start = (chip_at(j) * 2 + c) * block + h * half + p * TILE
@@ -243,21 +239,16 @@
         j = (0, 0, behind[d])[stage]
         h = (d, 1 - d, d)[stage]
         at = lat.at[lat_rows(j, core, h, p)]
-        return remote(at, at, ring_s.at[d, n % PIECES], ag_r.at[d, stage, p], neighbour[d])
-
-    def gather_wait(d, stage, p):
-        j = (behind[d], behind[d], opposite)[stage]
-        h = (d, 1 - d, d)[stage]
-        at = lat.at[lat_rows(j, core, h, p)]
-        remote(at, at, ring_s.at[d, 0], ag_r.at[d, stage, p], neighbour[d]).wait_recv()
+        return remote(at, at, ring_s.at[d, n % PIECES], ag_r.at[stage, p], neighbour[d])
+
+    def rows_wait(count, recv):
+        at = lat.at[pl.ds(0, count)]
+        remote(at, at, fw_s.at[0], recv, partner).wait_recv()
 
     def forward(j, h, p):
         at = lat.at[lat_rows(j, core, h, p)]
-        return remote(at, at, fw_s.at[0], fw_r.at[j, p], partner)
-
-    def forward_wait(j, p):
-        at = lat.at[pl.ds(0, 2 * TILE)]
-        remote(at, at, fw_s.at[0], fw_r.at[j, p], partner).wait_recv()
+        group = ((0, 0, 1, 1), (2, 2, 3, 3), (4, 4, 5, 5), (2, 2, 3, 3))[j][p]
+        return remote(at, at, fw_s.at[0], fw_r.at[group], partner)
 
     sent = ([], [])
 
@@ -271,7 +262,7 @@
     def send(d, make, *which):
         n = len(sent[d])
         if n >= PIECES:
-            drain(d, n - WINDOW + 1)
+            drain(d, n - WINDOWS[0 if n < 3 * PIECES else 1] + 1)
         copy = make(d, *which, n)
         copy.start()
         sent[d].append(copy)
@@ -298,6 +289,9 @@
     hid_loads[opposite].wait()
     for i in range(strips):
         strip_loads[i].wait()
+        if i == 0:
+            for copy in (*strip_loads[2:], *(hid_loads[j] for j in (1, 3, 0))):
+                copy.start()
         if i < strips - 1:
             down_strip(opposite, i, wdq[i], 0)
         else:
@@ -325,8 +319,8 @@
     for copy in late_loads:
         copy.wait()
 
-    for d in range(2):
-        pair_copy(toward[d]).wait_recv()
+    two = pair_in.at[pl.ds(0, 2)]
+    remote(two, two, pair_s.at[0], pair_r.at[1], partner).wait_recv()
     for p in range(PIECES):
         for d in range(2):
             h = 1 - d
@@ -335,8 +329,7 @@
                 ring_out[d, 1, rotary_tiles(1)] = rotary_sum(toward[d], h).astype(BF16)
             send(d, ring_copy, 1, p)
 
-    for d in range(2):
-        ring_first_wait(d)
+    tiles_wait(2 * (PIECES * tiles + 2), rs_first_r.at[0])
     for p in range(PIECES):
         for d in range(2):
             got = jnp.concatenate(
@@ -350,9 +343,8 @@
             send(d, ring_copy, 2, p)
 
     def totals(p):
+        tiles_wait(4 * (tiles + (2 if p == 0 else 0)), rs_r.at[p])
         for h in range(2):
-            ring_copy(1 - h, 1, p).wait_recv()
-            ring_copy(h, 2, p).wait_recv()
             total = row_sum(0, h * PIECES + p)
             total += ring_in[1 - h, 1, run_tiles(1, p)].astype(F32) + ring_in[h, 2, run_tiles(2, p)].astype(F32)
             at = lat_rows(0, core, h, p)
@@ -370,19 +362,17 @@
             send(d, gather_copy, stage, p)
 
     def near(stage, p):
+        rows_wait(2 * TILE, ag_r.at[stage, p])
         for d in range(2):
-            gather_wait(d, stage, p)
             forward(behind[d], (d, 1 - d)[stage], p).start()
 
     def far(p):
+        rows_wait(2 * TILE, ag_r.at[2, p])
         for d in range(2):
-            gather_wait(d, 2, p)
             forward(opposite, d, p).start()
 
-    def ready(offsets, first, count):
-        for p in range(first, first + count):
-            for j in offsets:
-                forward_wait(j, p)
+    def ready(group, offsets, first, count):
+        rows_wait(len(offsets) * count * 2 * TILE, fw_r.at[group])
         return piece_blocks(chip, block, offsets, first, count)
 
     pair_copy(0).wait_recv()
@@ -391,13 +381,13 @@
     totals(1)
     sends(1, 0)
     totals(2)
-    own = ready((0,), 0, 2)
+    own = ready(0, (0,), 0, 2)
     queries_in(own)
     keys_values_in(own)
     sends(0, 1)
     totals(3)
     sends(1, 1)
-    own = ready((0,), 2, 2)
+    own = ready(1, (0,), 2, 2)
     queries_in(own)
     keys_values_in(own)
     sends(0, 2)
@@ -407,10 +397,17 @@
     sends(0, 3)
     near(0, 1)
     sends(1, 3)
+    sends(2, 0)
     near(1, 1)
-    near_rows = ready((1, 3), 0, 2)
+    sends(2, 1)
+    near_rows = ready(2, (1, 3), 0, 2)
     queries_in(near_rows)
-    sends(2, 0)
+    near(0, 2)
+    sends(2, 2)
+    near(1, 2)
+    near(0, 3)
+    sends(2, 3)
+    near(1, 3)
     keys_values_in(near_rows)
     for h in range(2):
         total = rotary_sum(0, h)
@@ -424,23 +421,13 @@
             keyrow[low : low + TILE, :] = turned
             keyrow[low + TILE : low + 2 * TILE, :] = pltpu.roll(turned, ROPE, 1)
     keybuf[...] = keyrow[...].T[:ROPE].astype(BF16)
-    sends(2, 1)
-    near(0, 2)
-    sends(2, 2)
-    near(1, 2)
-    near(0, 3)
-    sends(2, 3)
-    near_rows = ready((1, 3), 2, 1)
+    near_rows = ready(3, (1, 3), 2, 2)
     queries_in(near_rows)
-    keys_values_in(near_rows)
-    near(1, 3)
     far(0)
-    near_rows = ready((1, 3), 3, 1)
-    queries_in(near_rows)
     far(1)
     keys_values_in(near_rows)
     far(2)
-    far_rows = ready((opposite,), 0, 2)
+    far_rows = ready(4, (opposite,), 0, 2)
     queries_in(far_rows)
     far(3)
     keys_values_in(far_rows)
@@ -449,9 +436,8 @@
     for d in range(2):
         drain(d, len(sent[d]))
     whole = lat.at[pl.ds(0, CHIPS * block)]
-    remote(whole, whole, fw_s.at[0], fw_r.at[0, 0], partner).wait_send()
-    for p in range(PIECES // 2, PIECES):
-        forward_wait(opposite, p)
+    remote(whole, whole, fw_s.at[0], fw_r.at[0], partner).wait_send()
+    ready(5, (opposite,), 2, 2)
 
 
 def store(q, kv, key, lat, wuq, wukv, tab, q_out, kv_out, key_out, qlast, kvlast, sem):
@@ -522,9 +508,9 @@
             pltpu.VMEM((2, 3, PIECES * tiles + 2, TILE, LANES), BF16),
             pltpu.VMEM((block, LANES), F32),
             dma((13,)),
-            dma((4,)), dma((1,)), dma((CHIPS,)),
-            dma((2, PIECES)), dma((2,)), dma((2, 2, PIECES)), dma((2, 3, PIECES)),
-            dma((1,)), dma((CHIPS, PIECES)),
+            dma((4,)), dma((1,)), dma((2,)),
+            dma((2, PIECES)), dma((1,)), dma((PIECES,)), dma((3, PIECES)),
+            dma((1,)), dma((6,)),
         ],
         compiler_params=pltpu.CompilerParams(
             collective_id=0, has_side_effects=True, vmem_limit_bytes=47_000_000

time: 84.8 us -> 84.2 us (level)
  no operation moved by 1% of the time
where the time goes in v4:
time: 84.2 us; the launch traced here: 83.9 us
  Pallas kernels  83.3 us (99%)
    pallas_call x1, Pallas kernels, shards(): pl.pallas_call(kernel, out_shape=(*(pltpu.VMEM(shape, BF16) for shape in...  80.3 us
    pallas_call x1, Pallas kernels, shards(): pl.pallas_call(store, out_shape=tuple((jax.ShapeDtypeStruct(shape, BF16)...  2.99 us

profile of v4, /device:TPU:43, one launch (start us, length us, event | category | flops | bytes accessed | tf_op | source)
XLA Modules:
  0.0 83.9 jit_solution(12097484230100599350)
XLA Ops:
  0.6 80.3 %shard_map.103 = (bf16[1024,1536]{1,0:T(8,128)(2,1)S(1)}, bf16[1024,2048]{1,0:T(8,128)(2,1)S(1)}, bf16[64,128]{1,0:T(8,128)(2,1)S(1)}, bf16[1024,2048]{1,0:T(8,1...) custom-call(bf16[1024,896]{1,0:T(8,128)(2,1)} %hidden.1, ...), custom_call_target="tpu_custom_call" | custom-call | flops 10854858752 | bytes 13000000 | tf_op jit(solution)/shard_map/pallas_call | solution.py:488
  80.9 3.0 %shard_map.104 = (bf16[1024,1536]{1,0:T(8,128)(2,1)}, bf16[1024,2048]{1,0:T(8,128)(2,1)}, bf16[64,128]{1,0:T(8,128)(2,1)}) custom-call(bf16[1024,1536]{1,0:T(8,128)(2,1)S(1)} %get-tuple-element.13.q, bf16[1024,2048]{1,0:T(8,128)(2,1)S(1)} %get-tuple-element.14.kv, bf16[64,128]{1,0:T(8,128)(2,1)S(1)} %get-tuple-element.15.key, ...), custom_call_target="tpu_custom_call" | custom-call | flops 678428672 | bytes 7400000 | tf_op jit(solution)/shard_map/pallas_call | solution.py:522
